TPU v7x, 32 devices: a whole 2x2x4 slice. The times are simulated.
32 devices in a mesh: seq: 8 (over z, x), grp: 4 (over y, core).
Axes of the slice: x: 2, y: 2, z: 4, core: 2. Of those that a mesh axis runs over, the one named last changes fastest.
Arguments:
- delta_codes: int32 [16, 16, 2048, 128], P('grp', None, 'seq'), may hold values from -63 to 63, as said below
- scale_index: int32 [16, 16, 128], P('grp', None, 'seq'), may hold values from 0 to 15
- anchor_codes: int32 [16, 16, 128], P('grp'), may hold values from -8 to 7
- scale_table: float32 [16, 128], replicated, may hold values from 5e-05 to 0.0005
- anchor_scale: float32 [128], replicated, may hold values from 0.0001 to 0.001
Outputs:
- decode_cache: bfloat16 [4, 64, 2048, 128], P('grp', 'seq')
Inputs may be any that keep to these rules, and one draw needn't show every extreme that they name: `delta_codes`: for every sequence, head and channel, the running sum of the codes from the sequence's first token lies in -32 .. 31 after every token, and in -2 .. 1 after the last token of each group of 16 tokens.
All inputs are finite; a program needn't handle non-finite values.
Results may differ from a plain program's by a relative error of at most 0.001.
Values may be sent and summed in bfloat16 or wider, within the bound.
A program may use at most 128 MiB of HBM per device.

v0:
```python
import functools

import jax
import jax.numpy as jnp
from jax import lax
from jax.experimental import pallas as pl
from jax.experimental.pallas import tpu as pltpu
from jax.sharding import PartitionSpec as P

MESH = pl.DeviceIdType.MESH
CHUNKS = 4
LAG = 1
HIGHEST = lax.Precision.HIGHEST


def exchange(
    codes, index_hbm, anchor_hbm, table_hbm, anchor_scale_hbm,
    landed, scales_ref, base_ref,
    raw, sums, relay, index_out, index_in, anchor_out, anchor_in,
    load_sem, send_sem, recv_sem, isend_sem, irecv_sem, asend_sem, arecv_sem,
    relay_sem, forward_sem,
    index_ref, anchor_ref, table_ref, anchor_scale_ref, small_sem,
):
    seqs, grps = lax.axis_size("seq"), lax.axis_size("grp")
    s, g = lax.axis_index("seq"), lax.axis_index("grp")
    blocks, rows, tokens, channels = sums.shape
    heads = codes.shape[1] // grps
    per_grp = blocks // grps
    half = grps // 2
    partner = lax.rem(g + half, grps)
    chunks = relay.shape[1]
    chunk_rows = rows // chunks
    passed = blocks // 2 * chunks
    seq_rows, head_rows = max(1, rows // heads), min(rows, heads)
    levels = table_ref.shape[0]
    groups = index_hbm.shape[2]
    group_len = tokens // groups

    def place_from(d, own):
        e = d // 2
        side = lax.rem(own // half + 1 + d, 2)
        h = side * half + lax.rem(own + e // per_grp, half)
        i = lax.rem(s + e, per_grp)
        first = i * rows
        return h, own * per_grp + i, first // heads, h * heads + lax.rem(first, heads)

    def place(d):
        return place_from(d, g)

    def is_me(d):
        h, to_s, _, _ = place(d)
        return jnp.logical_and(h == g, to_s == s)

    def load(d):
        _, _, b0, k0 = place(d)
        return pltpu.make_async_copy(
            codes.at[pl.ds(b0, seq_rows), pl.ds(k0, head_rows)], raw.at[d], load_sem.at[d]
        )

    def remote(src, dst, ssem, rsem, d):
        h, to_s, _, _ = place(d)
        return pltpu.make_async_remote_copy(
            src_ref=src, dst_ref=dst, send_sem=ssem, recv_sem=rsem,
            device_id={"seq": to_s, "grp": h}, device_id_type=MESH,
        )

    def window(j):
        return landed.at[:, pl.ds(pl.multiple_of(j * tokens, tokens), tokens), :]

    def send_sums(d):
        return remote(sums.at[d], window(s), send_sem.at[d], recv_sem.at[s], d)

    def at_partner(d):
        h, to_s, _, _ = place(d)
        return jnp.logical_and(h == partner, to_s == s)

    def part(c):
        return pl.ds(c * chunk_rows, chunk_rows)

    def send_relay(e, c):
        return pltpu.make_async_remote_copy(
            src_ref=sums.at[2 * e, part(c)], dst_ref=relay.at[e, c],
            send_sem=send_sem.at[2 * e], recv_sem=relay_sem.at[e, c],
            device_id={"seq": s, "grp": partner}, device_id_type=MESH,
        )

    def send_part(d, c):
        span = pl.ds(pl.multiple_of(s * tokens, tokens), tokens)
        return remote(
            sums.at[d, part(c)], landed.at[part(c), span, :], send_sem.at[d], recv_sem.at[s], d
        )

    def relayed(e):
        h, to_s, _, _ = place_from(2 * e, partner)
        return jnp.logical_not(jnp.logical_and(h == g, to_s == s))

    def forward(e, c):
        h, to_s, _, _ = place_from(2 * e, partner)
        span = pl.ds(pl.multiple_of(s * tokens, tokens), tokens)
        return pltpu.make_async_remote_copy(
            src_ref=relay.at[e, c], dst_ref=landed.at[pl.ds(c * chunk_rows, chunk_rows), span, :],
            send_sem=forward_sem.at[e], recv_sem=recv_sem.at[s],
            device_id={"seq": to_s, "grp": h}, device_id_type=MESH,
        )

    def pass_on(n):
        e, c = n // chunks, lax.rem(n, chunks)

        @pl.when(relayed(e))
        def _():
            send_relay(e, c).wait_recv()
            forward(e, c).start()

    def send_index(d):
        return remote(index_out.at[d], index_in.at[s], isend_sem.at[d], irecv_sem.at[s], d)

    def send_anchor(d):
        return remote(anchor_out.at[d], anchor_in, asend_sem.at[d], arecv_sem, d)

    ahead = min(2, blocks)
    for d in range(ahead):
        load(d).start()

    small = (
        (index_hbm, index_ref), (anchor_hbm, anchor_ref),
        (table_hbm, table_ref), (anchor_scale_hbm, anchor_scale_ref),
    )
    fetches = [
        pltpu.make_async_copy(src, dst, small_sem.at[n]) for n, (src, dst) in enumerate(small)
    ]
    for fetch in fetches:
        fetch.start()

    barrier = pltpu.get_barrier_semaphore()
    from_g = s // per_grp

    inside = lax.rem(from_g, half) == lax.rem(g, half)

    @pl.loop(0, 2 * seqs)
    def _(n):
        j = n // 2
        to_g = lax.rem(from_g + lax.rem(n, 2) * half, grps)

        @pl.when(jnp.logical_not(jnp.logical_and(j == s, to_g == g)))
        def _():
            pl.semaphore_signal(
                barrier, inc=1, device_id={"seq": j, "grp": to_g}, device_id_type=MESH
            )

    @pl.when(jnp.logical_not(inside))
    def _():
        pl.semaphore_signal(
            barrier, inc=1, device_id={"seq": s, "grp": partner}, device_id_type=MESH
        )

    expected = 2 * blocks + jnp.where(inside, -1, 1)

    t_out = lax.broadcasted_iota(jnp.int32, (tokens, tokens), 0)
    t_in = lax.broadcasted_iota(jnp.int32, (tokens, tokens), 1)
    same = t_out // group_len == t_in // group_len
    within = jnp.where(jnp.logical_and(same, t_out >= t_in), 1.0, 0.0).astype(jnp.bfloat16)

    @pl.loop(0, blocks)
    def _(d):
        load(d).wait()

        @pl.when(d + ahead < blocks)
        def _():
            load(d + ahead).start()

        away = jnp.logical_not(is_me(d))
        via = jnp.logical_and(lax.rem(d, 2) == 0, jnp.logical_not(at_partner(d)))
        straight = jnp.logical_and(away, jnp.logical_not(via))
        for c in range(chunks):
            for r in range(c * chunk_rows, (c + 1) * chunk_rows):
                x = raw[d, r // head_rows, r % head_rows].astype(jnp.float32).astype(jnp.bfloat16)
                run = jnp.dot(within, x, preferred_element_type=jnp.float32)
                sums[d, r] = run.astype(jnp.bfloat16)

            if c == 0:
                @pl.when(d == 0)
                def _():
                    pl.semaphore_wait(barrier, expected)

            @pl.when(via)
            def _():
                send_relay(d // 2, c).start()

            @pl.when(straight)
            def _():
                send_part(d, c).start()

        @pl.when(jnp.logical_and(d >= LAG, d - LAG < passed))
        def _():
            pass_on(d - LAG)

    for fetch in fetches:
        fetch.wait()

    @pl.loop(0, blocks)
    def _(d):
        _, _, b0, k0 = place(d)
        for b in range(seq_rows):
            these = pl.ds(b * head_rows, head_rows)
            index_out[d, these, :] = index_ref[b0 + b, pl.ds(k0, head_rows), :]
            anchor_out[d, these, :] = anchor_ref[b0 + b, pl.ds(k0, head_rows), :]

        @pl.when(jnp.logical_not(is_me(d)))
        def _():
            send_index(d).start()

            @pl.when(s == 0)
            def _():
                send_anchor(d).start()

    @pl.loop(min(blocks - LAG, passed), passed)
    def _(n):
        pass_on(n)

    @pl.loop(0, blocks)
    def _(d):
        @pl.when(is_me(d))
        def _():
            index_in[s] = index_out[d]
            for r in range(rows):
                landed[r, pl.ds(pl.multiple_of(s * tokens, tokens), tokens), :] = sums[d, r]

            @pl.when(s == 0)
            def _():
                anchor_in[...] = anchor_out[d]

    mine = jnp.logical_and(from_g == g, s == 0)

    @pl.when(jnp.logical_not(mine))
    def _():
        send_anchor(0).wait_recv()

    for r in range(rows):
        base_ref[r] = anchor_in[pl.ds(r, 1), :].astype(jnp.float32) * anchor_scale_ref[...]

    def from_me(j):
        return jnp.logical_and(j == s, from_g == g)

    @pl.loop(0, seqs)
    def _(j):
        @pl.when(jnp.logical_not(from_me(j)))
        def _():
            remote(index_out.at[0], index_in.at[j], isend_sem.at[0], irecv_sem.at[j], 0).wait_recv()

        table = table_ref[...]
        for r in range(rows):
            ids = jnp.broadcast_to(index_in[j, pl.ds(r, 1), :], (levels, groups))
            hot = (ids == lax.broadcasted_iota(jnp.int32, (levels, groups), 0)).astype(jnp.float32)
            found = lax.dot_general(
                hot, table, (((0,), (0,)), ((), ())),
                precision=HIGHEST, preferred_element_type=jnp.float32,
            )
            scales_ref[r, pl.ds(pl.multiple_of(j * groups, groups), groups), :] = found

    @pl.loop(0, seqs)
    def _(j):
        @pl.when(jnp.logical_not(from_me(j)))
        def _():
            remote(sums.at[0], window(j), send_sem.at[0], recv_sem.at[j], 0).wait_recv()

    @pl.loop(0, blocks)
    def _(d):
        @pl.when(jnp.logical_not(is_me(d)))
        def _():
            send_index(d).wait_send()

            @pl.when(s == 0)
            def _():
                send_anchor(d).wait_send()

            send_sums(d).wait_send()

    @pl.loop(0, blocks // 2)
    def _(e):
        @pl.when(relayed(e))
        def _():
            for c in range(chunks):
                forward(e, c).wait_send()


def rebuild(sums_ref, scales_ref, base_ref, out_hbm, built, out_sem):
    many, length, channels = built.shape
    groups = scales_ref.shape[1]
    group_len = length // groups
    stores = [pltpu.make_async_copy(built.at[r], out_hbm.at[0, r], out_sem.at[r]) for r in range(many)]
    for r in range(many):

        def step(j, base, r=r):
            at = pl.multiple_of(j * group_len, group_len)
            x = sums_ref[r, pl.ds(at, group_len), :].astype(jnp.float32)
            grown = x * scales_ref[r, pl.ds(j, 1), :]
            built[r, pl.ds(at, group_len), :] = (grown + base).astype(jnp.bfloat16)
            return base + grown[group_len - 1:]

        lax.fori_loop(0, groups, step, base_ref[r], unroll=16)
        stores[r].start()
    for copy in stores:
        copy.wait()


def on_device(delta_codes, scale_index, anchor_codes, scale_table, anchor_scale):
    seqs, grps = lax.axis_size("seq"), lax.axis_size("grp")
    seq_local, kv_heads, tokens, channels = delta_codes.shape
    groups = scale_index.shape[2]
    heads = kv_heads // grps
    rows = seq_local * grps * heads // seqs
    blocks = seq_local * kv_heads // rows
    seq_rows, head_rows = max(1, rows // heads), min(rows, heads)
    chunks = min(rows, CHUNKS)
    length = seqs * tokens
    vmem = pl.BlockSpec(memory_space=pltpu.VMEM)
    hbm = pl.BlockSpec(memory_space=pltpu.HBM)
    sums, scales, base = pl.pallas_call(
        exchange,
        out_shape=(
            jax.ShapeDtypeStruct((rows, length, channels), jnp.bfloat16),
            jax.ShapeDtypeStruct((rows, seqs * groups, channels), jnp.float32),
            jax.ShapeDtypeStruct((rows, 1, channels), jnp.float32),
        ),
        in_specs=[hbm] * 5,
        out_specs=(vmem, vmem, vmem),
        scratch_shapes=[
            pltpu.VMEM((blocks, seq_rows, head_rows, tokens, channels), jnp.int32),
            pltpu.VMEM((blocks, rows, tokens, channels), jnp.bfloat16),
            pltpu.VMEM((blocks // 2, chunks, rows // chunks, tokens, channels), jnp.bfloat16),
            pltpu.VMEM((blocks, rows, groups), jnp.int32),
            pltpu.VMEM((seqs, rows, groups), jnp.int32),
            pltpu.VMEM((blocks, rows, channels), jnp.int32),
            pltpu.VMEM((rows, channels), jnp.int32),
            pltpu.SemaphoreType.DMA((blocks,)),
            pltpu.SemaphoreType.DMA((blocks,)),
            pltpu.SemaphoreType.DMA((seqs,)),
            pltpu.SemaphoreType.DMA((blocks,)),
            pltpu.SemaphoreType.DMA((seqs,)),
            pltpu.SemaphoreType.DMA((blocks,)),
            pltpu.SemaphoreType.DMA,
            pltpu.SemaphoreType.DMA((blocks // 2, chunks)),
            pltpu.SemaphoreType.DMA((blocks // 2,)),
            pltpu.VMEM(scale_index.shape, jnp.int32),
            pltpu.VMEM(anchor_codes.shape, jnp.int32),
            pltpu.VMEM(scale_table.shape, jnp.float32),
            pltpu.VMEM((1, channels), jnp.float32),
            pltpu.SemaphoreType.DMA((4,)),
        ],
        compiler_params=pltpu.CompilerParams(
            collective_id=0, has_side_effects=True, vmem_limit_bytes=48 * 1024 * 1024
        ),
        name="exchange",
    )(delta_codes, scale_index, anchor_codes, scale_table, anchor_scale[None])

    out = pl.pallas_call(
        rebuild,
        out_shape=jax.ShapeDtypeStruct((1, rows, length, channels), jnp.bfloat16),
        in_specs=[vmem] * 3,
        out_specs=hbm,
        scratch_shapes=[
            pltpu.VMEM(sums.shape, jnp.bfloat16),
            pltpu.SemaphoreType.DMA((rows,)),
        ],
        compiler_params=pltpu.CompilerParams(vmem_limit_bytes=16 * 1024 * 1024),
        name="rebuild",
    )(sums, scales, base)
    return out


def solution(mesh):
    placed = (P("grp", None, "seq", None), P("grp", None, "seq"), P("grp", None, None), P(), P())
    return jax.shard_map(
        on_device,
        mesh=mesh,
        in_specs=placed,
        out_specs=P("grp", "seq", None, None),
        check_vma=False,
    )
```

profile of v0, /device:TPU:6, one launch (start us, length us, event | category | flops | bytes accessed | tf_op | source)
XLA Modules:
  0.0 106.5 jit_solution(15752198297326599527)
XLA Ops:
  0.0 0.0 copy-start
  0.0 0.8 copy-done
  0.8 0.0 copy-start.1
  0.8 0.8 copy-done.1
  1.5 0.0 copy-start.2
  1.5 0.7 copy-done.2
  2.2 0.0 copy-start.3
  2.2 0.7 copy-done.3
  2.9 100.3 %exchange.1 = (bf16[8,2048,128]{2,1,0:T(8,128)(2,1)S(1)}, f32[8,128,128]{2,1,0:T(8,128)S(1)}, f32[8,1,128]{2,1,0:T(1,128)S(1)}) custom-call(s32[4,16,256,128]{3,2,1,0:T(8,128)} %codes.1, s32[4,16,16]{2,1,0:T(8,128)S(1)} %copy-done, s32[4,16,128]{2,1,0:T(8,128)S(1)} %copy-done.1, f32[16,128]{1,0:T(8,128)S(1)} %copy-done.2, f32[1,128]{1,0:T(1,128)S(1)} %bitcast.1), custom_call_target="tpu_custom_call" | custom-call | tf_op jit(solution)/shard_map/exchange/pallas_call | solution.py:318
  103.1 3.3 %rebuild.1 = bf16[1,8,2048,128]{3,2,1,0:T(8,128)(2,1)} custom-call(bf16[8,2048,128]{2,1,0:T(8,128)(2,1)S(1)} %get-tuple-element.8.sums_ref, f32[8,128,128]{2,1,0:T(8,128)S(1)} %get-tuple-element.9.scales_ref, f32[8,1,128]{2,1,0:T(1,128)S(1)} %get-tuple-element.10.base_ref), custom_call_target="tpu_custom_call" | custom-call | tf_op jit(solution)/shard_map/rebuild/pallas_call | solution.py:356
Async XLA Ops:
  0.0 0.8 copy-start
  0.8 0.8 copy-start.1
  1.5 0.7 copy-start.2
  2.2 0.7 copy-start.3
where the time goes:
time: 109 us; the launch traced here: 106 us
  Pallas kernels  104 us (95%)
  local copies, waits for them, and re-layouts  2.87 us (3%)
    pallas_call x1, Pallas kernels, on_device(): pl.pallas_call(exchange, out_shape=(jax.ShapeDtypeStruct((rows, length, c...  100 us
    pallas_call x1, Pallas kernels, on_device(): pl.pallas_call(rebuild, out_shape=jax.ShapeDtypeStruct((1, rows, length,...  3.33 us
    unnamed x8, local copies, waits for them, and re-layouts  2.87 us

commit v1 on v0

--- a/solution.py
+++ b/solution.py
@@ -351,7 +351,7 @@
             collective_id=0, has_side_effects=True, vmem_limit_bytes=48 * 1024 * 1024
         ),
         name="exchange",
-    )(delta_codes, scale_index, anchor_codes, scale_table, anchor_scale[None])
+    )(*(pltpu.with_memory_space_constraint(a, pltpu.HBM) for a in (delta_codes, scale_index, anchor_codes, scale_table, anchor_scale[None])))
 
     out = pl.pallas_call(
         rebuild,

time: 109 us -> 105 us (0.963)
  local copies, waits for them, and re-layouts: 2.87 us -> 0 us
    unnamed x8 -> x0, local copies, waits for them, and re-layouts: 2.87 us -> none
where the time goes in v1:
time: 105 us; the launch traced here: 103 us
  Pallas kernels  103 us (98%)
    pallas_call x1, Pallas kernels, on_device(): pl.pallas_call(exchange, out_shape=(jax.ShapeDtypeStruct((rows, length, c...  100 us
    pallas_call x1, Pallas kernels, on_device(): pl.pallas_call(rebuild, out_shape=jax.ShapeDtypeStruct((1, rows, length,...  3.33 us

profile of v1, /device:TPU:6, one launch (start us, length us, event | category | flops | bytes accessed | tf_op | source)
XLA Modules:
  0.0 103.4 jit_solution(11905318316793246880)
XLA Ops:
  0.0 100.1 %exchange.1 = (bf16[8,2048,128]{2,1,0:T(8,128)(2,1)S(1)}, f32[8,128,128]{2,1,0:T(8,128)S(1)}, f32[8,1,128]{2,1,0:T(1,128)S(1)}) custom-call(s32[4,16,256,128]{3,2,1,0:T(8,128)} %codes.1, s32[4,16,16]{2,1,0:T(8,128)} %index_hbm.1, s32[4,16,128]{2,1,0:T(8,128)} %anchor_hbm.1, f32[16,128]{1,0:T(8,128)} %table_hbm.1, f32[1,128]{1,0:T(1,128)} %bitcast.1), custom_call_target="tpu_custom_call" | custom-call | tf_op jit(solution)/shard_map/exchange/pallas_call | solution.py:318
  100.1 3.3 %rebuild.1 = bf16[1,8,2048,128]{3,2,1,0:T(8,128)(2,1)} custom-call(bf16[8,2048,128]{2,1,0:T(8,128)(2,1)S(1)} %get-tuple-element.8.sums_ref, f32[8,128,128]{2,1,0:T(8,128)S(1)} %get-tuple-element.9.scales_ref, f32[8,1,128]{2,1,0:T(1,128)S(1)} %get-tuple-element.10.base_ref), custom_call_target="tpu_custom_call" | custom-call | tf_op jit(solution)/shard_map/rebuild/pallas_call | solution.py:356

commit v2 on v1

v2 whole, which is shorter than its diff:
```python
import jax
import jax.numpy as jnp
from jax import lax
from jax.experimental import pallas as pl
from jax.experimental.pallas import tpu as pltpu
from jax.sharding import PartitionSpec as P

MESH = pl.DeviceIdType.MESH
MOVED = (1,)
SMALL = 6
LEAD = 0
LAG = 4
KEEP = 1
HIGHEST = lax.Precision.HIGHEST


def grow(landed, scales_ref, base_ref, r):
    groups = scales_ref.shape[1]
    group_len = landed.shape[1] // groups

    def step(j, base):
        at = pl.multiple_of(j * group_len, group_len)
        x = landed[r, pl.ds(at, group_len), :].astype(jnp.float32)
        grown = x * scales_ref[r, pl.ds(j, 1), :]
        return at, (grown + base).astype(jnp.bfloat16), base + grown[group_len - 1:]

    return groups, step


def exchange(
    codes, index_hbm, anchor_hbm, table_hbm, anchor_scale_hbm,
    landed, scales_ref, base_ref,
    raw, sums, relay, index_out, index_hold, index_in, anchor_out, anchor_in,
    first_sem, load_sem, send_sem, recv_sem, ihold_sem, irecv_sem, arecv_sem,
    relay_half_sem, relay_sem,
    index_ref, anchor_ref, table_ref, anchor_scale_ref, small_sem, wide_ref,
):
    seqs, grps = lax.axis_size("seq"), lax.axis_size("grp")
    s, g = lax.axis_index("seq"), lax.axis_index("grp")
    blocks, rows, tokens, channels = sums.shape
    heads = codes.shape[1] // grps
    per_grp = blocks // grps
    half = grps // 2
    partner = lax.rem(g + half, grps)
    seq_rows, head_rows = raw.shape[0], raw.shape[2]
    levels = table_ref.shape[0]
    groups = index_hbm.shape[2]
    group_len = tokens // groups
    piece = tokens // 2
    zone = s // per_grp
    zone_partner = lax.rem(zone + half, grps)
    via = zone != g
    pass_on = zone != partner
    mine = zone == g
    also = jnp.logical_and
    chunks = rows + 1

    def place_from(d, own):
        side, e, i = lax.rem(d, 2), lax.rem(d // 2, half), d // 2 // half
        h = lax.rem(own // half + 1 + side, 2) * half + lax.rem(own + e, half)
        first = i * rows
        return h, own * per_grp + i, first // heads, h * heads + lax.rem(first, heads)

    def is_me(d):
        h, to_s, _, _ = place_from(d, g)
        return also(h == g, to_s == s)

    def load(d, b, sem):
        _, _, b0, k0 = place_from(d, g)
        return pltpu.make_async_copy(codes.at[b0 + b, pl.ds(k0, head_rows)], raw.at[b, d], sem)

    def loaded(b, i):
        skip = 1 if b == 0 and i == 0 else 0
        these = raw.at[b, pl.ds(i * 2 * half + skip, 2 * half - skip)]
        return pltpu.make_async_copy(these, these, load_sem.at[b, i])

    def spot(r, lo, size):
        return landed.at[r, pl.ds(pl.multiple_of(s * tokens + lo, size), size), :]

    def remote(src, dst, rsem, h, to_s):
        return pltpu.make_async_remote_copy(
            src_ref=src, dst_ref=dst, send_sem=send_sem, recv_sem=rsem,
            device_id={"seq": to_s, "grp": h}, device_id_type=MESH,
        )

    def here(ref, rsem):
        return remote(ref, ref, rsem, g, s)

    def relay_sem_at(d, r, lo, size):
        if size == tokens:
            return relay_sem.at[d // 2 // half, r - 1]
        return relay_half_sem.at[d // 2, lo // piece]

    def send_relay(d, r, lo, size):
        return remote(
            sums.at[d, r, pl.ds(lo, size)], relay.at[d // 2, r, pl.ds(lo, size)],
            relay_sem_at(d, r, lo, size), partner, s,
        )

    def send_part(d, r, lo, size):
        h, to_s, _, _ = place_from(d, g)
        return remote(sums.at[d, r, pl.ds(lo, size)], spot(r, lo, size), recv_sem.at[r], h, to_s)

    def forward(d, r, lo, size):
        h, to_s, _, _ = place_from(d, partner)
        return remote(
            relay.at[d // 2, r, pl.ds(lo, size)], spot(r, lo, size), recv_sem.at[r], h, to_s
        )

    def send_index(d):
        h, to_s, _, _ = place_from(d, g)
        return remote(index_out.at[d], index_in.at[s], irecv_sem, h, to_s)

    def hold_index(d):
        return remote(index_out.at[d], index_hold.at[d // 2], ihold_sem, partner, s)

    def forward_index(d):
        h, to_s, _, _ = place_from(d, partner)
        return remote(index_hold.at[d // 2], index_in.at[s], irecv_sem, h, to_s)

    def send_anchor(d):
        h, to_s, _, _ = place_from(d, g)
        return remote(anchor_out.at[d], anchor_in, arecv_sem, h, to_s)

    def sends_anchor(d):
        _, to_s, _, _ = place_from(d, g)
        return also(to_s == s, jnp.logical_not(is_me(d)))

    load(0, 0, first_sem).start()
    barrier = pltpu.get_barrier_semaphore()

    @pl.loop(0, seqs)
    def _(j):
        straight = jnp.logical_or(zone // half == g // half, j // per_grp == zone)
        to_g = jnp.where(straight, zone, zone_partner)

        @pl.when(jnp.logical_not(also(j == s, to_g == g)))
        def _():
            pl.semaphore_signal(
                barrier, inc=1, device_id={"seq": j, "grp": to_g}, device_id_type=MESH
            )

    @pl.when(pass_on)
    def _():
        pl.semaphore_signal(
            barrier, inc=1, device_id={"seq": s, "grp": partner}, device_id_type=MESH
        )

    @pl.when(also(g == zone_partner, lax.rem(s, per_grp) == 0))
    def _():
        @pl.loop(0, seqs if MOVED else 0)
        def _(j):
            @pl.when(j // per_grp != zone)
            def _():
                pl.semaphore_signal(
                    barrier, inc=1, device_id={"seq": j, "grp": zone}, device_id_type=MESH
                )

    expected = (
        blocks // 2
        + jnp.where(via, 1 + (1 if MOVED else 0), blocks // 2 - 1)
        + jnp.where(pass_on, blocks // 2, 0)
    )

    for b in range(seq_rows):
        @pl.loop(1 if b == 0 else 0, blocks)
        def _(d, b=b):
            load(d, b, load_sem.at[b, d // (2 * half)]).start()

    small = (
        (index_hbm, index_ref), (anchor_hbm, anchor_ref),
        (table_hbm, table_ref), (anchor_scale_hbm, anchor_scale_ref),
    )
    fetches = [
        pltpu.make_async_copy(src, dst, small_sem.at[n]) for n, (src, dst) in enumerate(small)
    ]
    for fetch in fetches:
        fetch.start()

    t_out = lax.broadcasted_iota(jnp.int32, (tokens, tokens), 0)
    t_in = lax.broadcasted_iota(jnp.int32, (tokens, tokens), 1)
    same = t_out // group_len == t_in // group_len
    within = jnp.where(also(same, t_out >= t_in), 1.0, 0.0).astype(jnp.bfloat16)

    def compute(d, r, lo, size):
        x = raw[r // head_rows, d, lax.rem(r, head_rows), pl.ds(lo, size), :]
        x = x.astype(jnp.float32).astype(jnp.bfloat16)
        run = jnp.dot(within[:size, :size], x, preferred_element_type=jnp.float32)
        sums[d, r, pl.ds(lo, size), :] = run.astype(jnp.bfloat16)

    def is_moved(e, i, lo, size):
        hit = size == piece and e == 0 and lo // piece in MOVED
        return i == 0 if hit else i < 0

    def send_all(i, r, lo, size):
        for e in range(half):
            d = (i * half + e) * 2
            if e == 0 and size == piece and lo == 0:
                @pl.when(i > 0)
                def _():
                    compute(d, r, lo, size)
            else:
                compute(d, r, lo, size)

            relayed = also(via, jnp.logical_not(is_moved(e, i, lo, size)))

            @pl.when(relayed)
            def _(d=d):
                send_relay(d, r, lo, size).start()

            @pl.when(jnp.logical_not(relayed))
            def _(d=d):
                send_part(d, r, lo, size).start()

        for e in range(half):
            d = (i * half + e) * 2 + 1
            compute(d, r, lo, size)

            @pl.when(jnp.logical_not(is_me(d)))
            def _(d=d):
                send_part(d, r, lo, size).start()

    def forward_all(i, r, lo, size):
        def from_relay(e):
            d = (i * half + e) * 2
            forward(d, r, lo, size).start()

        if size == tokens:
            both = relay.at[pl.ds(i * half, half), r]
            here(both, relay_sem.at[i, r - 1]).wait_recv()
            for e in range(half):
                from_relay(e)
        else:
            for e in range(half):
                @pl.when(jnp.logical_not(is_moved(e, i, lo, size)))
                def _(e=e):
                    send_relay((i * half + e) * 2, r, lo, size).wait_recv()
                    from_relay(e)

    lane = lax.broadcasted_iota(jnp.int32, (groups, rows * groups), 1)
    spread = (lax.rem(lane, groups) == lax.broadcasted_iota(jnp.int32, lane.shape, 0))
    lane = lax.broadcasted_iota(jnp.int32, (rows, rows * groups), 1)
    own_row = lane // groups == lax.broadcasted_iota(jnp.int32, lane.shape, 0)

    def send_small():
        for fetch in fetches:
            fetch.wait()

        ids = index_ref[...].astype(jnp.float32).astype(jnp.bfloat16)
        ids = ids.reshape(-1, groups)
        wide = jnp.dot(ids, spread.astype(jnp.bfloat16), preferred_element_type=jnp.float32)
        wide_ref[...] = wide.reshape(wide_ref.shape)

        @pl.loop(0, blocks)
        def _(d):
            _, _, b0, k0 = place_from(d, g)
            line = 0.0
            for b in range(seq_rows):
                these = pl.ds(b * head_rows, head_rows)
                anchor_out[d, these, :] = anchor_ref[b0 + b, pl.ds(k0, head_rows), :]
                kept = jnp.where(own_row[b * head_rows:(b + 1) * head_rows],
                                 wide_ref[b0 + b, pl.ds(k0, head_rows), :], 0.0)
                line += jnp.sum(kept, axis=0, keepdims=True)
            index_out[d] = line.astype(jnp.int32)

            relayed = also(lax.rem(d, 2) == 0, via)

            @pl.when(relayed)
            def _():
                hold_index(d).start()

            @pl.when(jnp.logical_not(jnp.logical_or(relayed, is_me(d))))
            def _():
                send_index(d).start()

            @pl.when(sends_anchor(d))
            def _():
                send_anchor(d).start()

    steps = (chunks + LEAD * (per_grp - 1)) * per_grp
    pltpu.make_async_copy(raw.at[0, 0], raw.at[0, 0], first_sem).wait()
    compute(0, 0, 0, piece)
    pl.semaphore_wait(barrier, expected)

    def at_chunk(n, ready, do):
        i = lax.rem(n, per_grp)
        c = n // per_grp - LEAD * i
        for lo in (0, piece):
            @pl.when(also(ready, c == lo // piece))
            def _(lo=lo):
                do(i, 0, lo, piece)

        @pl.when(also(ready, also(c >= 2, c < chunks)))
        def _():
            do(i, c - 1, 0, tokens)

    def wait_and_send(i, r, lo, size):
        if lo == 0:
            for b in range(seq_rows):
                for k in range(per_grp):
                    @pl.when(also(i == k, r == b * head_rows))
                    def _(b=b, k=k):
                        loaded(b, k).wait()
        send_all(i, r, lo, size)

    @pl.loop(0, steps + LAG)
    def _(n):
        at_chunk(jnp.maximum(n - LAG, 0), also(n >= LAG, pass_on), forward_all)
        at_chunk(n, n < steps, wait_and_send)

        @pl.when(n == SMALL)
        def _():
            send_small()

        @pl.when(also(pass_on, n == SMALL + LAG))
        def _():
            here(index_hold, ihold_sem).wait_recv()

            @pl.loop(0, blocks // 2)
            def _(e):
                forward_index(e * 2).start()

    @pl.loop(0, blocks)
    def _(d):
        @pl.when(is_me(d))
        def _():
            index_in[s] = index_out[d]
            anchor_in[...] = anchor_out[d]
            for r in range(rows):
                landed[r, pl.ds(pl.multiple_of(s * tokens, tokens), tokens), :] = sums[d, r]

    def fewer(ref, sem, axis):
        def part(count):
            at = [slice(None)] * (axis + 1)
            at[axis] = pl.ds(0, count)
            return ref.at[tuple(at)]

        size = ref.shape[axis]

        @pl.when(mine)
        def _():
            here(part(size - size // seqs), sem).wait_recv()

        @pl.when(jnp.logical_not(mine))
        def _():
            here(ref, sem).wait_recv()

    @pl.when(jnp.logical_not(mine))
    def _():
        here(anchor_in, arecv_sem).wait_recv()

    for r in range(rows):
        base_ref[r] = anchor_in[pl.ds(r, 1), :].astype(jnp.float32) * anchor_scale_ref[...]

    fewer(index_in, irecv_sem, 0)

    @pl.loop(0, seqs)
    def _(j):
        many = rows * groups
        ids = jnp.broadcast_to(index_in[j], (levels, many))
        hot = (ids == lax.broadcasted_iota(jnp.int32, (levels, many), 0)).astype(jnp.float32)
        found = lax.dot_general(
            hot, table_ref[...], (((0,), (0,)), ((), ())),
            precision=HIGHEST, preferred_element_type=jnp.float32,
        )
        for r in range(rows):
            scales_ref[r, pl.ds(pl.multiple_of(j * groups, groups), groups), :] = (
                found[r * groups:(r + 1) * groups]
            )

    @pl.loop(0, rows)
    def _(r):
        fewer(landed.at[r], recv_sem.at[r], 0)

        @pl.when(r < rows - min(KEEP, rows))
        def _():
            many, step = grow(landed, scales_ref, base_ref, r)

            def put(j, base):
                at, built, base = step(j, base)
                landed[r, pl.ds(at, group_len), :] = built
                return base

            lax.fori_loop(0, many, put, base_ref[r], unroll=16)

    def sent(ref):
        here(ref, recv_sem.at[0]).wait_send()

    @pl.when(mine)
    def _():
        sent(sums.at[pl.ds(0, blocks - 1)])
        sent(index_out.at[pl.ds(0, blocks - 1)])
        for _ in range(grps - 1):
            sent(anchor_out.at[0])

    @pl.when(jnp.logical_not(mine))
    def _():
        sent(sums)
        sent(index_out)

    @pl.when(pass_on)
    def _():
        sent(index_hold)
        if MOVED:
            sent(relay.at[pl.ds(1, blocks // 2 - 1)])
            if rows > 1:
                sent(relay.at[0, pl.ds(1, rows - 1)])
            for _ in range(2 - len(MOVED)):
                sent(relay.at[0, 0, pl.ds(0, piece)])
        else:
            sent(relay)


def rebuild(landed, scales_ref, base_ref, out_hbm, built, out_sem):
    rows = landed.shape[0]
    keep = built.shape[0]
    done = rows - keep
    stores = []
    if done:
        stores.append(pltpu.make_async_copy(
            landed.at[pl.ds(0, done)], out_hbm.at[0, pl.ds(0, done)], out_sem.at[keep]
        ))
        stores[0].start()
    for q in range(keep):
        r = done + q
        many, step = grow(landed, scales_ref, base_ref, r)
        group_len = landed.shape[1] // many

        def put(j, base, q=q, step=step):
            at, grown, base = step(j, base)
            built[q, pl.ds(at, group_len), :] = grown
            return base

        lax.fori_loop(0, many, put, base_ref[r], unroll=16)
        stores.append(pltpu.make_async_copy(built.at[q], out_hbm.at[0, r], out_sem.at[q]))
        stores[-1].start()
    for store in stores:
        store.wait()


def on_device(delta_codes, scale_index, anchor_codes, scale_table, anchor_scale):
    seqs, grps = lax.axis_size("seq"), lax.axis_size("grp")
    seq_local, kv_heads, tokens, channels = delta_codes.shape
    groups = scale_index.shape[2]
    heads = kv_heads // grps
    rows = seq_local * grps * heads // seqs
    blocks = seq_local * kv_heads // rows
    seq_rows, head_rows = max(1, rows // heads), min(rows, heads)
    keep = min(KEEP, rows)
    length = seqs * tokens
    vmem = pl.BlockSpec(memory_space=pltpu.VMEM)
    hbm = pl.BlockSpec(memory_space=pltpu.HBM)
    operands = (delta_codes, scale_index, anchor_codes, scale_table, anchor_scale[None])
    landed, scales, base = pl.pallas_call(
        exchange,
        out_shape=(
            jax.ShapeDtypeStruct((rows, length, channels), jnp.bfloat16),
            jax.ShapeDtypeStruct((rows, seqs * groups, channels), jnp.float32),
            jax.ShapeDtypeStruct((rows, 1, channels), jnp.float32),
        ),
        in_specs=[hbm] * 5,
        out_specs=(vmem, vmem, vmem),
        scratch_shapes=[
            pltpu.VMEM((seq_rows, blocks, head_rows, tokens, channels), jnp.int32),
            pltpu.VMEM((blocks, rows, tokens, channels), jnp.bfloat16),
            pltpu.VMEM((blocks // 2, rows, tokens, channels), jnp.bfloat16),
            pltpu.VMEM((blocks, 1, rows * groups), jnp.int32),
            pltpu.VMEM((blocks // 2, 1, rows * groups), jnp.int32),
            pltpu.VMEM((seqs, 1, rows * groups), jnp.int32),
            pltpu.VMEM((blocks, rows, channels), jnp.int32),
            pltpu.VMEM((rows, channels), jnp.int32),
            pltpu.SemaphoreType.DMA,
            pltpu.SemaphoreType.DMA((seq_rows, blocks // grps)),
            pltpu.SemaphoreType.DMA,
            pltpu.SemaphoreType.DMA((rows,)),
            pltpu.SemaphoreType.DMA,
            pltpu.SemaphoreType.DMA,
            pltpu.SemaphoreType.DMA,
            pltpu.SemaphoreType.DMA((blocks // 2, 2)),
            pltpu.SemaphoreType.DMA((blocks // grps, max(1, rows - 1))),
            pltpu.VMEM(scale_index.shape, jnp.int32),
            pltpu.VMEM(anchor_codes.shape, jnp.int32),
            pltpu.VMEM(scale_table.shape, jnp.float32),
            pltpu.VMEM((1, channels), jnp.float32),
            pltpu.SemaphoreType.DMA((4,)),
            pltpu.VMEM(scale_index.shape[:2] + (rows * groups,), jnp.float32),
        ],
        compiler_params=pltpu.CompilerParams(
            collective_id=0, has_side_effects=True, vmem_limit_bytes=48 * 1024 * 1024
        ),
        name="exchange",
    )(*(pltpu.with_memory_space_constraint(x, pltpu.HBM) for x in operands))

    return pl.pallas_call(
        rebuild,
        out_shape=jax.ShapeDtypeStruct((1, rows, length, channels), jnp.bfloat16),
        in_specs=[vmem] * 3,
        out_specs=hbm,
        scratch_shapes=[
            pltpu.VMEM((keep, length, channels), jnp.bfloat16),
            pltpu.SemaphoreType.DMA((keep + 1,)),
        ],
        compiler_params=pltpu.CompilerParams(vmem_limit_bytes=16 * 1024 * 1024),
        name="rebuild",
    )(landed, scales, base)


def solution(mesh):
    placed = (P("grp", None, "seq", None), P("grp", None, "seq"), P("grp", None, None), P(), P())
    return jax.shard_map(
        on_device,
        mesh=mesh,
        in_specs=placed,
        out_specs=P("grp", "seq", None, None),
        check_vma=False,
    )
```

time: 105 us -> 99.6 us (0.949)
  Pallas kernels: 103 us -> 97.9 us
    pallas_call x1, Pallas kernels: 100 us -> 95.9 us  [on_device(): pl.pallas_call(exchange, out_shape=(jax.ShapeDtypeStruct((rows, length, c...]
    pallas_call x1, Pallas kernels: 3.33 us -> 2.02 us  [on_device(): pl.pallas_call(rebuild, out_shape=jax.ShapeDtypeStruct((1, rows, length,...]
where the time goes in v2:
time: 99.6 us; the launch traced here: 97.9 us
  Pallas kernels  97.9 us (98%)
    pallas_call x1, Pallas kernels, on_device(): pl.pallas_call(exchange, out_shape=(jax.ShapeDtypeStruct((rows, length, c...  95.9 us
    pallas_call x1, Pallas kernels, on_device(): pl.pallas_call(rebuild, out_shape=jax.ShapeDtypeStruct((1, rows, length,...  2.02 us

profile of v2, /device:TPU:6, one launch (start us, length us, event | category | flops | bytes accessed | tf_op | source)
XLA Modules:
  0.0 97.9 jit_solution(11476721110303149620)
XLA Ops:
  0.0 95.9 %exchange.1 = (bf16[8,2048,128]{2,1,0:T(8,128)(2,1)S(1)}, f32[8,128,128]{2,1,0:T(8,128)S(1)}, f32[8,1,128]{2,1,0:T(1,128)S(1)}) custom-call(s32[4,16,256,128]{3,2,1,0:T(8,128)} %codes.1, s32[4,16,16]{2,1,0:T(8,128)} %index_hbm.1, s32[4,16,128]{2,1,0:T(8,128)} %anchor_hbm.1, f32[16,128]{1,0:T(8,128)} %table_hbm.1, f32[1,128]{1,0:T(1,128)} %bitcast.1), custom_call_target="tpu_custom_call" | custom-call | tf_op jit(solution)/shard_map/exchange/pallas_call | solution.py:454
  95.9 2.0 %rebuild.1 = bf16[1,8,2048,128]{3,2,1,0:T(8,128)(2,1)} custom-call(bf16[8,2048,128]{2,1,0:T(8,128)(2,1)S(1)} %get-tuple-element.8.landed, f32[8,128,128]{2,1,0:T(8,128)S(1)} %get-tuple-element.9.scales_ref, f32[8,1,128]{2,1,0:T(1,128)S(1)} %get-tuple-element.10.base_ref), custom_call_target="tpu_custom_call" | custom-call | tf_op jit(solution)/shard_map/rebuild/pallas_call | solution.py:494

commit v3 on v2

--- a/solution.py
+++ b/solution.py
@@ -10,6 +10,7 @@
 SMALL = 6
 LEAD = 0
 LAG = 4
+RELAY_LAG = 1
 KEEP = 1
 HIGHEST = lax.Precision.HIGHEST
 
@@ -27,11 +28,15 @@
     return groups, step
 
 
+def arrival_cuts(rows):
+    return sorted({0, rows // 2, rows - min(KEEP, rows), rows})
+
+
 def exchange(
     codes, index_hbm, anchor_hbm, table_hbm, anchor_scale_hbm,
     landed, scales_ref, base_ref,
     raw, sums, relay, index_out, index_hold, index_in, anchor_out, anchor_in,
-    first_sem, load_sem, send_sem, recv_sem, ihold_sem, irecv_sem, arecv_sem,
+    first_sem, rest_sem, load_sem, send_sem, recv_sem, ihold_sem, irecv_sem, arecv_sem,
     relay_half_sem, relay_sem,
     index_ref, anchor_ref, table_ref, anchor_scale_ref, small_sem, wide_ref,
 ):
@@ -54,10 +59,18 @@
     mine = zone == g
     also = jnp.logical_and
     chunks = rows + 1
+    cuts = arrival_cuts(rows)
+
+    def arrival_sem(r):
+        group = 0
+        for at in cuts[1:-1]:
+            group = group + jnp.where(r >= at, 1, 0)
+        return recv_sem.at[group]
+
 
     def place_from(d, own):
         side, e, i = lax.rem(d, 2), lax.rem(d // 2, half), d // 2 // half
-        h = lax.rem(own // half + 1 + side, 2) * half + lax.rem(own + e, half)
+        h = lax.rem(own // half + 1 + side, 2) * half + lax.rem(e + i, half)
         first = i * rows
         return h, own * per_grp + i, first // heads, h * heads + lax.rem(first, heads)
 
@@ -70,8 +83,7 @@
         return pltpu.make_async_copy(codes.at[b0 + b, pl.ds(k0, head_rows)], raw.at[b, d], sem)
 
     def loaded(b, i):
-        skip = 1 if b == 0 and i == 0 else 0
-        these = raw.at[b, pl.ds(i * 2 * half + skip, 2 * half - skip)]
+        these = raw.at[b, pl.ds(i * 2 * half, 2 * half)]
         return pltpu.make_async_copy(these, these, load_sem.at[b, i])
 
     def spot(r, lo, size):
@@ -99,12 +111,12 @@
 
     def send_part(d, r, lo, size):
         h, to_s, _, _ = place_from(d, g)
-        return remote(sums.at[d, r, pl.ds(lo, size)], spot(r, lo, size), recv_sem.at[r], h, to_s)
+        return remote(sums.at[d, r, pl.ds(lo, size)], spot(r, lo, size), arrival_sem(r), h, to_s)
 
     def forward(d, r, lo, size):
         h, to_s, _, _ = place_from(d, partner)
         return remote(
-            relay.at[d // 2, r, pl.ds(lo, size)], spot(r, lo, size), recv_sem.at[r], h, to_s
+            relay.at[d // 2, r, pl.ds(lo, size)], spot(r, lo, size), arrival_sem(r), h, to_s
         )
 
     def send_index(d):
@@ -126,7 +138,21 @@
         _, to_s, _, _ = place_from(d, g)
         return also(to_s == s, jnp.logical_not(is_me(d)))
 
-    load(0, 0, first_sem).start()
+    ahead = 2 * half
+
+    def first_rows(d, lo, size, sem):
+        _, _, b0, k0 = place_from(d, g)
+        return pltpu.make_async_copy(
+            codes.at[b0, pl.ds(k0 + lo, size)], raw.at[0, d, pl.ds(lo, size)], sem
+        )
+
+    def first_loaded(lo, size, sem):
+        these = raw.at[0, pl.ds(0, ahead), pl.ds(lo, size)]
+        return pltpu.make_async_copy(these, these, sem)
+
+    for d in range(ahead):
+        first_rows(d, 0, 1, first_sem).start()
+
     barrier = pltpu.get_barrier_semaphore()
 
     @pl.loop(0, seqs)
@@ -146,7 +172,9 @@
             barrier, inc=1, device_id={"seq": s, "grp": partner}, device_id_type=MESH
         )
 
-    @pl.when(also(g == zone_partner, lax.rem(s, per_grp) == 0))
+    gets_moved = also(g // half == zone_partner // half, lax.rem(g, half) == 0)
+
+    @pl.when(also(gets_moved, lax.rem(s, per_grp) == 0))
     def _():
         @pl.loop(0, seqs if MOVED else 0)
         def _(j):
@@ -162,20 +190,19 @@
         + jnp.where(pass_on, blocks // 2, 0)
     )
 
+    if head_rows > 1:
+        for d in range(ahead):
+            first_rows(d, 1, head_rows - 1, rest_sem).start()
+
     for b in range(seq_rows):
-        @pl.loop(1 if b == 0 else 0, blocks)
+        @pl.loop(ahead if b == 0 else 0, blocks)
         def _(d, b=b):
             load(d, b, load_sem.at[b, d // (2 * half)]).start()
 
-    small = (
-        (index_hbm, index_ref), (anchor_hbm, anchor_ref),
-        (table_hbm, table_ref), (anchor_scale_hbm, anchor_scale_ref),
-    )
-    fetches = [
-        pltpu.make_async_copy(src, dst, small_sem.at[n]) for n, (src, dst) in enumerate(small)
-    ]
-    for fetch in fetches:
-        fetch.start()
+    fetch_index = pltpu.make_async_copy(index_hbm, index_ref, small_sem.at[0])
+    fetch_anchor = pltpu.make_async_copy(anchor_hbm, anchor_ref, small_sem.at[1])
+    fetch_index.start()
+    fetch_anchor.start()
 
     t_out = lax.broadcasted_iota(jnp.int32, (tokens, tokens), 0)
     t_in = lax.broadcasted_iota(jnp.int32, (tokens, tokens), 1)
@@ -188,21 +215,29 @@
         run = jnp.dot(within[:size, :size], x, preferred_element_type=jnp.float32)
         sums[d, r, pl.ds(lo, size), :] = run.astype(jnp.bfloat16)
 
-    def is_moved(e, i, lo, size):
+    def moves(own):
+        up = zone // half < own // half
+        last = also(zone == grps - 1, lax.rem(own, half) == half - 1)
+        return jnp.logical_or(up, lax.rem(own, half) == 0)
+
+    def is_moved(own, e, i, lo, size):
         hit = size == piece and e == 0 and lo // piece in MOVED
-        return i == 0 if hit else i < 0
+        return also(i == 0, moves(own)) if hit else i < 0
 
     def send_all(i, r, lo, size):
+        def compute_all():
+            for side in range(2):
+                for e in range(half):
+                    compute((i * half + e) * 2 + side, r, lo, size)
+
+        if size == piece and lo == 0:
+            pl.when(i > 0)(compute_all)
+        else:
+            compute_all()
+
         for e in range(half):
             d = (i * half + e) * 2
-            if e == 0 and size == piece and lo == 0:
-                @pl.when(i > 0)
-                def _():
-                    compute(d, r, lo, size)
-            else:
-                compute(d, r, lo, size)
-
-            relayed = also(via, jnp.logical_not(is_moved(e, i, lo, size)))
+            relayed = also(via, jnp.logical_not(is_moved(g, e, i, lo, size)))
 
             @pl.when(relayed)
             def _(d=d):
@@ -214,7 +249,6 @@
 
         for e in range(half):
             d = (i * half + e) * 2 + 1
-            compute(d, r, lo, size)
 
             @pl.when(jnp.logical_not(is_me(d)))
             def _(d=d):
@@ -232,7 +266,7 @@
                 from_relay(e)
         else:
             for e in range(half):
-                @pl.when(jnp.logical_not(is_moved(e, i, lo, size)))
+                @pl.when(jnp.logical_not(is_moved(partner, e, i, lo, size)))
                 def _(e=e):
                     send_relay((i * half + e) * 2, r, lo, size).wait_recv()
                     from_relay(e)
@@ -243,8 +277,8 @@
     own_row = lane // groups == lax.broadcasted_iota(jnp.int32, lane.shape, 0)
 
     def send_small():
-        for fetch in fetches:
-            fetch.wait()
+        fetch_index.wait()
+        fetch_anchor.wait()
 
         ids = index_ref[...].astype(jnp.float32).astype(jnp.bfloat16)
         ids = ids.reshape(-1, groups)
@@ -278,8 +312,9 @@
                 send_anchor(d).start()
 
     steps = (chunks + LEAD * (per_grp - 1)) * per_grp
-    pltpu.make_async_copy(raw.at[0, 0], raw.at[0, 0], first_sem).wait()
-    compute(0, 0, 0, piece)
+    first_loaded(0, 1, first_sem).wait()
+    for d in range(ahead):
+        compute(d, 0, 0, piece)
     pl.semaphore_wait(barrier, expected)
 
     def at_chunk(n, ready, do):
@@ -296,16 +331,24 @@
 
     def wait_and_send(i, r, lo, size):
         if lo == 0:
+            if head_rows > 1:
+                @pl.when(also(i == 0, r == 1))
+                def _():
+                    first_loaded(1, head_rows - 1, rest_sem).wait()
+
             for b in range(seq_rows):
-                for k in range(per_grp):
+                for k in range(1 if b == 0 else 0, per_grp):
                     @pl.when(also(i == k, r == b * head_rows))
                     def _(b=b, k=k):
                         loaded(b, k).wait()
         send_all(i, r, lo, size)
 
+    lag = jnp.where(zone // half == g // half, RELAY_LAG, LAG)
+
     @pl.loop(0, steps + LAG)
     def _(n):
-        at_chunk(jnp.maximum(n - LAG, 0), also(n >= LAG, pass_on), forward_all)
+        m = n - lag
+        at_chunk(jnp.maximum(m, 0), also(also(m >= 0, m < steps), pass_on), forward_all)
         at_chunk(n, n < steps, wait_and_send)
 
         @pl.when(n == SMALL)
@@ -319,6 +362,11 @@
             @pl.loop(0, blocks // 2)
             def _(e):
                 forward_index(e * 2).start()
+
+    fetch_table = pltpu.make_async_copy(table_hbm, table_ref, small_sem.at[0])
+    fetch_scale = pltpu.make_async_copy(anchor_scale_hbm, anchor_scale_ref, small_sem.at[1])
+    fetch_table.start()
+    fetch_scale.start()
 
     @pl.loop(0, blocks)
     def _(d):
@@ -329,30 +377,25 @@
             for r in range(rows):
                 landed[r, pl.ds(pl.multiple_of(s * tokens, tokens), tokens), :] = sums[d, r]
 
-    def fewer(ref, sem, axis):
-        def part(count):
-            at = [slice(None)] * (axis + 1)
-            at[axis] = pl.ds(0, count)
-            return ref.at[tuple(at)]
-
-        size = ref.shape[axis]
-
+    def fewer(part, size, sem):
         @pl.when(mine)
         def _():
             here(part(size - size // seqs), sem).wait_recv()
 
         @pl.when(jnp.logical_not(mine))
         def _():
-            here(ref, sem).wait_recv()
+            here(part(size), sem).wait_recv()
 
     @pl.when(jnp.logical_not(mine))
     def _():
         here(anchor_in, arecv_sem).wait_recv()
 
+    fetch_table.wait()
+    fetch_scale.wait()
     for r in range(rows):
         base_ref[r] = anchor_in[pl.ds(r, 1), :].astype(jnp.float32) * anchor_scale_ref[...]
 
-    fewer(index_in, irecv_sem, 0)
+    fewer(lambda size: index_in.at[pl.ds(0, size)], seqs, irecv_sem)
 
     @pl.loop(0, seqs)
     def _(j):
@@ -368,12 +411,12 @@
                 found[r * groups:(r + 1) * groups]
             )
 
-    @pl.loop(0, rows)
-    def _(r):
-        fewer(landed.at[r], recv_sem.at[r], 0)
-
-        @pl.when(r < rows - min(KEEP, rows))
-        def _():
+    def finish(group, first, last):
+        many_rows = pl.ds(first, last - first)
+        fewer(lambda size: landed.at[many_rows, pl.ds(0, size)], seqs * tokens, recv_sem.at[group])
+
+        @pl.loop(first, min(last, rows - min(KEEP, rows)))
+        def _(r):
             many, step = grow(landed, scales_ref, base_ref, r)
 
             def put(j, base):
@@ -382,6 +425,9 @@
                 return base
 
             lax.fori_loop(0, many, put, base_ref[r], unroll=16)
+
+    for group, first in enumerate(cuts[:-1]):
+        finish(group, first, cuts[group + 1])
 
     def sent(ref):
         here(ref, recv_sem.at[0]).wait_send()
@@ -405,8 +451,10 @@
             sent(relay.at[pl.ds(1, blocks // 2 - 1)])
             if rows > 1:
                 sent(relay.at[0, pl.ds(1, rows - 1)])
-            for _ in range(2 - len(MOVED)):
-                sent(relay.at[0, 0, pl.ds(0, piece)])
+            for k in range(2):
+                @pl.when(jnp.logical_not(is_moved(partner, 0, 0, k * piece, piece)))
+                def _(k=k):
+                    sent(relay.at[0, 0, pl.ds(k * piece, piece)])
         else:
             sent(relay)
 
@@ -417,9 +465,8 @@
     done = rows - keep
     stores = []
     if done:
-        stores.append(pltpu.make_async_copy(
-            landed.at[pl.ds(0, done)], out_hbm.at[0, pl.ds(0, done)], out_sem.at[keep]
-        ))
+        these = pl.ds(0, done)
+        stores.append(pltpu.make_async_copy(landed.at[these], out_hbm.at[0, these], out_sem.at[keep]))
         stores[0].start()
     for q in range(keep):
         r = done + q
@@ -470,9 +517,10 @@
             pltpu.VMEM((blocks, rows, channels), jnp.int32),
             pltpu.VMEM((rows, channels), jnp.int32),
             pltpu.SemaphoreType.DMA,
+            pltpu.SemaphoreType.DMA,
             pltpu.SemaphoreType.DMA((seq_rows, blocks // grps)),
             pltpu.SemaphoreType.DMA,
-            pltpu.SemaphoreType.DMA((rows,)),
+            pltpu.SemaphoreType.DMA((len(arrival_cuts(rows)) - 1,)),
             pltpu.SemaphoreType.DMA,
             pltpu.SemaphoreType.DMA,
             pltpu.SemaphoreType.DMA,
@@ -482,7 +530,7 @@
             pltpu.VMEM(anchor_codes.shape, jnp.int32),
             pltpu.VMEM(scale_table.shape, jnp.float32),
             pltpu.VMEM((1, channels), jnp.float32),
-            pltpu.SemaphoreType.DMA((4,)),
+            pltpu.SemaphoreType.DMA((2,)),
             pltpu.VMEM(scale_index.shape[:2] + (rows * groups,), jnp.float32),
         ],
         compiler_params=pltpu.CompilerParams(

time: 99.6 us -> 99 us (level); the launches traced: 97.9 us -> 98.8 us
  no operation moved by 1% of the time
where the time goes in v3:
time: 99 us; the launch traced here: 98.8 us
  Pallas kernels  98.8 us (100%)
    pallas_call x1, Pallas kernels, on_device(): pl.pallas_call(exchange, out_shape=(jax.ShapeDtypeStruct((rows, length, c...  96.8 us
    pallas_call x1, Pallas kernels, on_device(): pl.pallas_call(rebuild, out_shape=jax.ShapeDtypeStruct((1, rows, length,...  2.02 us

profile of v3, /device:TPU:6, one launch (start us, length us, event | category | flops | bytes accessed | tf_op | source)
XLA Modules:
  0.0 98.8 jit_solution(3281368684591311902)
XLA Ops:
  0.0 96.8 %exchange.1 = (bf16[8,2048,128]{2,1,0:T(8,128)(2,1)S(1)}, f32[8,128,128]{2,1,0:T(8,128)S(1)}, f32[8,1,128]{2,1,0:T(1,128)S(1)}) custom-call(s32[4,16,256,128]{3,2,1,0:T(8,128)} %codes.1, s32[4,16,16]{2,1,0:T(8,128)} %index_hbm.1, s32[4,16,128]{2,1,0:T(8,128)} %anchor_hbm.1, f32[16,128]{1,0:T(8,128)} %table_hbm.1, f32[1,128]{1,0:T(1,128)} %bitcast.1), custom_call_target="tpu_custom_call" | custom-call | tf_op jit(solution)/shard_map/exchange/pallas_call | solution.py:501
  96.8 2.0 %rebuild.1 = bf16[1,8,2048,128]{3,2,1,0:T(8,128)(2,1)} custom-call(bf16[8,2048,128]{2,1,0:T(8,128)(2,1)S(1)} %get-tuple-element.8.landed, f32[8,128,128]{2,1,0:T(8,128)S(1)} %get-tuple-element.9.scales_ref, f32[8,1,128]{2,1,0:T(1,128)S(1)} %get-tuple-element.10.base_ref), custom_call_target="tpu_custom_call" | custom-call | tf_op jit(solution)/shard_map/rebuild/pallas_call | solution.py:542

commit v4 on v3

--- a/solution.py
+++ b/solution.py
@@ -10,6 +10,7 @@
 SMALL = 6
 LEAD = 0
 LAG = 4
+FIRST = 2
 RELAY_LAG = 1
 KEEP = 1
 HIGHEST = lax.Precision.HIGHEST
@@ -51,7 +52,8 @@
     levels = table_ref.shape[0]
     groups = index_hbm.shape[2]
     group_len = tokens // groups
-    piece = tokens // 2
+    piece = tokens // FIRST
+    halves = ((0, piece), (piece, tokens - piece))
     zone = s // per_grp
     zone_partner = lax.rem(zone + half, grps)
     via = zone != g
@@ -87,7 +89,7 @@
         return pltpu.make_async_copy(these, these, load_sem.at[b, i])
 
     def spot(r, lo, size):
-        return landed.at[r, pl.ds(pl.multiple_of(s * tokens + lo, size), size), :]
+        return landed.at[r, pl.ds(pl.multiple_of(s * tokens + lo, piece), size), :]
 
     def remote(src, dst, rsem, h, to_s):
         return pltpu.make_async_remote_copy(
@@ -101,7 +103,7 @@
     def relay_sem_at(d, r, lo, size):
         if size == tokens:
             return relay_sem.at[d // 2 // half, r - 1]
-        return relay_half_sem.at[d // 2, lo // piece]
+        return relay_half_sem.at[d // 2, 1 if lo else 0]
 
     def send_relay(d, r, lo, size):
         return remote(
@@ -150,27 +152,25 @@
         these = raw.at[0, pl.ds(0, ahead), pl.ds(lo, size)]
         return pltpu.make_async_copy(these, these, sem)
 
-    for d in range(ahead):
-        first_rows(d, 0, 1, first_sem).start()
-
     barrier = pltpu.get_barrier_semaphore()
-
-    @pl.loop(0, seqs)
-    def _(j):
-        straight = jnp.logical_or(zone // half == g // half, j // per_grp == zone)
-        to_g = jnp.where(straight, zone, zone_partner)
-
-        @pl.when(jnp.logical_not(also(j == s, to_g == g)))
-        def _():
-            pl.semaphore_signal(
-                barrier, inc=1, device_id={"seq": j, "grp": to_g}, device_id_type=MESH
-            )
 
     @pl.when(pass_on)
     def _():
         pl.semaphore_signal(
             barrier, inc=1, device_id={"seq": s, "grp": partner}, device_id_type=MESH
         )
+
+
+    @pl.loop(0, seqs)
+    def _(j):
+        straight = jnp.logical_or(zone // half == g // half, j // per_grp == zone)
+        to_g = jnp.where(straight, zone, zone_partner)
+
+        @pl.when(jnp.logical_not(also(j == s, to_g == g)))
+        def _():
+            pl.semaphore_signal(
+                barrier, inc=1, device_id={"seq": j, "grp": to_g}, device_id_type=MESH
+            )
 
     gets_moved = also(g // half == zone_partner // half, lax.rem(g, half) == 0)
 
@@ -184,6 +184,9 @@
                     barrier, inc=1, device_id={"seq": j, "grp": zone}, device_id_type=MESH
                 )
 
+    for d in range(ahead):
+        first_rows(d, 0, 1, first_sem).start()
+
     expected = (
         blocks // 2
         + jnp.where(via, 1 + (1 if MOVED else 0), blocks // 2 - 1)
@@ -221,7 +224,7 @@
         return jnp.logical_or(up, lax.rem(own, half) == 0)
 
     def is_moved(own, e, i, lo, size):
-        hit = size == piece and e == 0 and lo // piece in MOVED
+        hit = size < tokens and e == 0 and (1 if lo else 0) in MOVED
         return also(i == 0, moves(own)) if hit else i < 0
 
     def send_all(i, r, lo, size):
@@ -230,7 +233,7 @@
                 for e in range(half):
                     compute((i * half + e) * 2 + side, r, lo, size)
 
-        if size == piece and lo == 0:
+        if size < tokens and lo == 0:
             pl.when(i > 0)(compute_all)
         else:
             compute_all()
@@ -312,6 +315,7 @@
                 send_anchor(d).start()
 
     steps = (chunks + LEAD * (per_grp - 1)) * per_grp
+    small_at = min(SMALL, steps - 1)
     first_loaded(0, 1, first_sem).wait()
     for d in range(ahead):
         compute(d, 0, 0, piece)
@@ -320,10 +324,10 @@
     def at_chunk(n, ready, do):
         i = lax.rem(n, per_grp)
         c = n // per_grp - LEAD * i
-        for lo in (0, piece):
-            @pl.when(also(ready, c == lo // piece))
-            def _(lo=lo):
-                do(i, 0, lo, piece)
+        for k, (lo, size) in enumerate(halves):
+            @pl.when(also(ready, c == k))
+            def _(lo=lo, size=size):
+                do(i, 0, lo, size)
 
         @pl.when(also(ready, also(c >= 2, c < chunks)))
         def _():
@@ -351,11 +355,11 @@
         at_chunk(jnp.maximum(m, 0), also(also(m >= 0, m < steps), pass_on), forward_all)
         at_chunk(n, n < steps, wait_and_send)
 
-        @pl.when(n == SMALL)
+        @pl.when(n == small_at)
         def _():
             send_small()
 
-        @pl.when(also(pass_on, n == SMALL + LAG))
+        @pl.when(also(pass_on, n == small_at + LAG))
         def _():
             here(index_hold, ihold_sem).wait_recv()
 
@@ -451,10 +455,10 @@
             sent(relay.at[pl.ds(1, blocks // 2 - 1)])
             if rows > 1:
                 sent(relay.at[0, pl.ds(1, rows - 1)])
-            for k in range(2):
-                @pl.when(jnp.logical_not(is_moved(partner, 0, 0, k * piece, piece)))
-                def _(k=k):
-                    sent(relay.at[0, 0, pl.ds(k * piece, piece)])
+            for lo, size in halves:
+                @pl.when(jnp.logical_not(is_moved(partner, 0, 0, lo, size)))
+                def _(lo=lo, size=size):
+                    sent(relay.at[0, 0, pl.ds(lo, size)])
         else:
             sent(relay)
 

time: 99 us -> 99 us (level)
  no operation moved by 1% of the time
where the time goes in v4:
time: 99 us; the launch traced here: 98.8 us
  Pallas kernels  98.8 us (100%)
    pallas_call x1, Pallas kernels, on_device(): pl.pallas_call(exchange, out_shape=(jax.ShapeDtypeStruct((rows, length, c...  96.8 us
    pallas_call x1, Pallas kernels, on_device(): pl.pallas_call(rebuild, out_shape=jax.ShapeDtypeStruct((1, rows, length,...  2.02 us

profile of v4, /device:TPU:6, one launch (start us, length us, event | category | flops | bytes accessed | tf_op | source)
XLA Modules:
  0.0 98.8 jit_solution(13499307902614728058)
XLA Ops:
  0.0 96.8 %exchange.1 = (bf16[8,2048,128]{2,1,0:T(8,128)(2,1)S(1)}, f32[8,128,128]{2,1,0:T(8,128)S(1)}, f32[8,1,128]{2,1,0:T(1,128)S(1)}) custom-call(s32[4,16,256,128]{3,2,1,0:T(8,128)} %codes.1, s32[4,16,16]{2,1,0:T(8,128)} %index_hbm.1, s32[4,16,128]{2,1,0:T(8,128)} %anchor_hbm.1, f32[16,128]{1,0:T(8,128)} %table_hbm.1, f32[1,128]{1,0:T(1,128)} %bitcast.1), custom_call_target="tpu_custom_call" | custom-call | tf_op jit(solution)/shard_map/exchange/pallas_call | solution.py:505
  96.8 2.0 %rebuild.1 = bf16[1,8,2048,128]{3,2,1,0:T(8,128)(2,1)} custom-call(bf16[8,2048,128]{2,1,0:T(8,128)(2,1)S(1)} %get-tuple-element.8.landed, f32[8,128,128]{2,1,0:T(8,128)S(1)} %get-tuple-element.9.scales_ref, f32[8,1,128]{2,1,0:T(1,128)S(1)} %get-tuple-element.10.base_ref), custom_call_target="tpu_custom_call" | custom-call | tf_op jit(solution)/shard_map/rebuild/pallas_call | solution.py:546

commit v5 on v4

--- a/solution.py
+++ b/solution.py
@@ -300,6 +300,8 @@
                 line += jnp.sum(kept, axis=0, keepdims=True)
             index_out[d] = line.astype(jnp.int32)
 
+        @pl.loop(0, blocks)
+        def _(d):
             relayed = also(lax.rem(d, 2) == 0, via)
 
             @pl.when(relayed)

time: 99 us -> 99 us (level)
  no operation moved by 1% of the time
where the time goes in v5:
time: 99 us; the launch traced here: 98.8 us
  Pallas kernels  98.8 us (100%)
    pallas_call x1, Pallas kernels, on_device(): pl.pallas_call(exchange, out_shape=(jax.ShapeDtypeStruct((rows, length, c...  96.8 us
    pallas_call x1, Pallas kernels, on_device(): pl.pallas_call(rebuild, out_shape=jax.ShapeDtypeStruct((1, rows, length,...  2.02 us

profile of v5, /device:TPU:6, one launch (start us, length us, event | category | flops | bytes accessed | tf_op | source)
XLA Modules:
  0.0 98.8 jit_solution(8026305593413873613)
XLA Ops:
  0.0 96.8 %exchange.1 = (bf16[8,2048,128]{2,1,0:T(8,128)(2,1)S(1)}, f32[8,128,128]{2,1,0:T(8,128)S(1)}, f32[8,1,128]{2,1,0:T(1,128)S(1)}) custom-call(s32[4,16,256,128]{3,2,1,0:T(8,128)} %codes.1, s32[4,16,16]{2,1,0:T(8,128)} %index_hbm.1, s32[4,16,128]{2,1,0:T(8,128)} %anchor_hbm.1, f32[16,128]{1,0:T(8,128)} %table_hbm.1, f32[1,128]{1,0:T(1,128)} %bitcast.1), custom_call_target="tpu_custom_call" | custom-call | tf_op jit(solution)/shard_map/exchange/pallas_call | solution.py:507
  96.8 2.0 %rebuild.1 = bf16[1,8,2048,128]{3,2,1,0:T(8,128)(2,1)} custom-call(bf16[8,2048,128]{2,1,0:T(8,128)(2,1)S(1)} %get-tuple-element.8.landed, f32[8,128,128]{2,1,0:T(8,128)S(1)} %get-tuple-element.9.scales_ref, f32[8,1,128]{2,1,0:T(1,128)S(1)} %get-tuple-element.10.base_ref), custom_call_target="tpu_custom_call" | custom-call | tf_op jit(solution)/shard_map/rebuild/pallas_call | solution.py:548

commit v6 on v5

--- a/solution.py
+++ b/solution.py
@@ -9,10 +9,10 @@
 MOVED = (1,)
 SMALL = 6
 LEAD = 0
-LAG = 4
+LAG = 3
 FIRST = 2
 RELAY_LAG = 1
-KEEP = 1
+KEEP = 2
 HIGHEST = lax.Precision.HIGHEST
 
 
@@ -30,7 +30,7 @@
 
 
 def arrival_cuts(rows):
-    return sorted({0, rows // 2, rows - min(KEEP, rows), rows})
+    return sorted({0, rows - min(KEEP, rows), rows})
 
 
 def exchange(
@@ -202,8 +202,8 @@
         def _(d, b=b):
             load(d, b, load_sem.at[b, d // (2 * half)]).start()
 
-    fetch_index = pltpu.make_async_copy(index_hbm, index_ref, small_sem.at[0])
-    fetch_anchor = pltpu.make_async_copy(anchor_hbm, anchor_ref, small_sem.at[1])
+    fetch_index = pltpu.make_async_copy(index_hbm, index_ref, load_sem.at[0, 0])
+    fetch_anchor = pltpu.make_async_copy(anchor_hbm, anchor_ref, small_sem)
     fetch_index.start()
     fetch_anchor.start()
 
@@ -369,8 +369,8 @@
             def _(e):
                 forward_index(e * 2).start()
 
-    fetch_table = pltpu.make_async_copy(table_hbm, table_ref, small_sem.at[0])
-    fetch_scale = pltpu.make_async_copy(anchor_scale_hbm, anchor_scale_ref, small_sem.at[1])
+    fetch_table = pltpu.make_async_copy(table_hbm, table_ref, load_sem.at[0, 0])
+    fetch_scale = pltpu.make_async_copy(anchor_scale_hbm, anchor_scale_ref, small_sem)
     fetch_table.start()
     fetch_scale.start()
 
@@ -536,7 +536,7 @@
             pltpu.VMEM(anchor_codes.shape, jnp.int32),
             pltpu.VMEM(scale_table.shape, jnp.float32),
             pltpu.VMEM((1, channels), jnp.float32),
-            pltpu.SemaphoreType.DMA((2,)),
+            pltpu.SemaphoreType.DMA,
             pltpu.VMEM(scale_index.shape[:2] + (rows * groups,), jnp.float32),
         ],
         compiler_params=pltpu.CompilerParams(

time: 99 us -> 99 us (level)
  no operation moved by 1% of the time
where the time goes in v6:
time: 99 us; the launch traced here: 98.8 us
  Pallas kernels  98.8 us (100%)
    pallas_call x1, Pallas kernels, on_device(): pl.pallas_call(exchange, out_shape=(jax.ShapeDtypeStruct((rows, length, c...  96.8 us
    pallas_call x1, Pallas kernels, on_device(): pl.pallas_call(rebuild, out_shape=jax.ShapeDtypeStruct((1, rows, length,...  2.03 us

profile of v6, /device:TPU:6, one launch (start us, length us, event | category | flops | bytes accessed | tf_op | source)
XLA Modules:
  0.0 98.8 jit_solution(15149010155295051243)
XLA Ops:
  0.0 96.8 %exchange.1 = (bf16[8,2048,128]{2,1,0:T(8,128)(2,1)S(1)}, f32[8,128,128]{2,1,0:T(8,128)S(1)}, f32[8,1,128]{2,1,0:T(1,128)S(1)}) custom-call(s32[4,16,256,128]{3,2,1,0:T(8,128)} %codes.1, s32[4,16,16]{2,1,0:T(8,128)} %index_hbm.1, s32[4,16,128]{2,1,0:T(8,128)} %anchor_hbm.1, f32[16,128]{1,0:T(8,128)} %table_hbm.1, f32[1,128]{1,0:T(1,128)} %bitcast.1), custom_call_target="tpu_custom_call" | custom-call | tf_op jit(solution)/shard_map/exchange/pallas_call | solution.py:507
  96.8 2.0 %rebuild.1 = bf16[1,8,2048,128]{3,2,1,0:T(8,128)(2,1)} custom-call(bf16[8,2048,128]{2,1,0:T(8,128)(2,1)S(1)} %get-tuple-element.8.landed, f32[8,128,128]{2,1,0:T(8,128)S(1)} %get-tuple-element.9.scales_ref, f32[8,1,128]{2,1,0:T(1,128)S(1)} %get-tuple-element.10.base_ref), custom_call_target="tpu_custom_call" | custom-call | tf_op jit(solution)/shard_map/rebuild/pallas_call | solution.py:548

commit v7 on v5

--- a/solution.py
+++ b/solution.py
@@ -197,11 +197,12 @@
         for d in range(ahead):
             first_rows(d, 1, head_rows - 1, rest_sem).start()
 
-    for b in range(seq_rows):
-        @pl.loop(ahead if b == 0 else 0, blocks)
-        def _(d, b=b):
+    def load_all(b, first):
+        @pl.loop(first, blocks)
+        def _(d):
             load(d, b, load_sem.at[b, d // (2 * half)]).start()
 
+    load_all(0, ahead)
     fetch_index = pltpu.make_async_copy(index_hbm, index_ref, small_sem.at[0])
     fetch_anchor = pltpu.make_async_copy(anchor_hbm, anchor_ref, small_sem.at[1])
     fetch_index.start()
@@ -322,6 +323,8 @@
     for d in range(ahead):
         compute(d, 0, 0, piece)
     pl.semaphore_wait(barrier, expected)
+    for b in range(1, seq_rows):
+        load_all(b, 0)
 
     def at_chunk(n, ready, do):
         i = lax.rem(n, per_grp)

time: 99 us -> 99 us (level)
  no operation moved by 1% of the time
where the time goes in v7:
time: 99 us; the launch traced here: 98.8 us
  Pallas kernels  98.8 us (100%)
    pallas_call x1, Pallas kernels, on_device(): pl.pallas_call(exchange, out_shape=(jax.ShapeDtypeStruct((rows, length, c...  96.8 us
    pallas_call x1, Pallas kernels, on_device(): pl.pallas_call(rebuild, out_shape=jax.ShapeDtypeStruct((1, rows, length,...  2.02 us

profile of v7, /device:TPU:6, one launch (start us, length us, event | category | flops | bytes accessed | tf_op | source)
XLA Modules:
  0.0 98.8 jit_solution(17259043255509356904)
XLA Ops:
  0.0 96.8 %exchange.1 = (bf16[8,2048,128]{2,1,0:T(8,128)(2,1)S(1)}, f32[8,128,128]{2,1,0:T(8,128)S(1)}, f32[8,1,128]{2,1,0:T(1,128)S(1)}) custom-call(s32[4,16,256,128]{3,2,1,0:T(8,128)} %codes.1, s32[4,16,16]{2,1,0:T(8,128)} %index_hbm.1, s32[4,16,128]{2,1,0:T(8,128)} %anchor_hbm.1, f32[16,128]{1,0:T(8,128)} %table_hbm.1, f32[1,128]{1,0:T(1,128)} %bitcast.1), custom_call_target="tpu_custom_call" | custom-call | tf_op jit(solution)/shard_map/exchange/pallas_call | solution.py:510
  96.8 2.0 %rebuild.1 = bf16[1,8,2048,128]{3,2,1,0:T(8,128)(2,1)} custom-call(bf16[8,2048,128]{2,1,0:T(8,128)(2,1)S(1)} %get-tuple-element.8.landed, f32[8,128,128]{2,1,0:T(8,128)S(1)} %get-tuple-element.9.scales_ref, f32[8,1,128]{2,1,0:T(1,128)S(1)} %get-tuple-element.10.base_ref), custom_call_target="tpu_custom_call" | custom-call | tf_op jit(solution)/shard_map/rebuild/pallas_call | solution.py:551
